TPU v7x, 32 devices: a whole 2x2x4 slice. The times are simulated.
32 devices in a mesh: groups: 2 (over x), blk: 16 (over z, y, core).
Axes of the slice: x: 2, y: 2, z: 4, core: 2. Of those that a mesh axis runs over, the one named last changes fastest.
Arguments:
- queries: bfloat16 [4096, 4096], P(('groups', 'blk')), parts along dimension 0, may hold values from -96 to 96
- keys: bfloat16 [4096, 512], P(('groups', 'blk')), parts along dimension 0, may hold values from -3 to 3
- values: bfloat16 [4096, 512], P(('groups', 'blk')), parts along dimension 0, may hold values from -4 to 4
- out_packed: int32 [4096, 512], P('blk'), may hold values from -2147483648 to 2147483646
- out_scales: bfloat16 [32, 4096], replicated, may hold values from 0.0029907227 to 0.029907227
- hadamard_signs: int32 [4096], replicated, may hold values from 0 to 1
Outputs:
- mixed: bfloat16 [4096, 4096], P(('groups', 'blk')), parts along dimension 0
There are 2 independent parts, one for each index of `groups`. A program takes and returns all parts, laid end to end along the dimension named above; an argument that names none is the same for every part. Nothing has to cross between parts.
All inputs are finite; a program needn't handle non-finite values.
Results may differ from a plain program's by a relative error of at most 0.012.
Values may be sent and summed in bfloat16 or wider, within the bound.
A program may use at most 256 MiB of HBM per device.

v0:
```python
import math

import jax
import jax.numpy as jnp
from jax import lax
from jax.sharding import PartitionSpec as P

HEAD_SIZE = 128
QUERY_HEADS = 32
KEY_VALUE_HEADS = 4
GROUP = 128


masked_fill_value = -1e30


def sylvester(block_count):
    index = jnp.arange(block_count, dtype=jnp.int32)
    both = jnp.bitwise_and(index[:, None], index[None, :])
    parity = jnp.zeros((block_count, block_count), jnp.int32)
    for bit_number in range(block_count.bit_length() - 1):
        parity = jnp.bitwise_xor(parity, jnp.bitwise_and(jnp.right_shift(both, bit_number), 1))
    return (1 - 2 * parity).astype(jnp.bfloat16)


def rotate(attention, hadamard_signs):
    block_count = attention.shape[0]
    signed = (attention * (2 * hadamard_signs - 1).astype(jnp.bfloat16)).reshape(
        block_count, QUERY_HEADS, HEAD_SIZE
    )
    outer = jnp.einsum(
        "gh,rhd->rgd", sylvester(QUERY_HEADS), signed, preferred_element_type=jnp.float32
    )
    upper = outer.astype(jnp.bfloat16)
    lower = (outer - upper.astype(jnp.float32)).astype(jnp.bfloat16)
    inner_table = sylvester(HEAD_SIZE)
    inner = jnp.einsum("rgd,de->rge", upper, inner_table, preferred_element_type=jnp.float32)
    inner = inner + jnp.einsum(
        "rgd,de->rge", lower, inner_table, preferred_element_type=jnp.float32
    )
    return (
        (inner * (1.0 / math.sqrt(QUERY_HEADS * HEAD_SIZE)))
        .reshape(block_count, QUERY_HEADS * HEAD_SIZE)
        .astype(jnp.bfloat16)
    )


def dequantize_rows(packed, out_scales):
    block_count = packed.shape[0]
    group_count = out_scales.shape[0]
    group_index = jnp.arange(block_count, dtype=jnp.int32) // GROUP
    member = (group_index[:, None] == jnp.arange(group_count, dtype=jnp.int32)[None, :]).astype(
        jnp.bfloat16
    )
    scale_rows = jnp.dot(member, out_scales, preferred_element_type=jnp.float32)
    fields = [jnp.bitwise_and(jnp.right_shift(packed, 4 * nibble), 15) for nibble in range(8)]
    levels = jnp.concatenate(fields, axis=1) - 8
    return (levels.astype(jnp.float32) * scale_rows).astype(jnp.bfloat16)


def update(state, query_tile, query_positions, key_block, value_block, key_positions):
    largest, totals, summed = state
    scores = jnp.einsum("qkgd,nkd->kgqn", query_tile, key_block, preferred_element_type=jnp.float32)
    scores = scores * (1.0 / math.sqrt(HEAD_SIZE))
    allowed = query_positions[:, None] >= key_positions[None, :]
    scores = jnp.where(allowed, scores, masked_fill_value)
    new_largest = jnp.maximum(largest, jnp.max(scores, axis=-1))
    fading = jnp.exp(largest - new_largest)
    weights = jnp.exp(scores - new_largest[..., None])
    totals = totals * fading + jnp.sum(weights, axis=-1)
    product = jnp.einsum(
        "kgqn,nkd->qkgd",
        weights.astype(jnp.bfloat16),
        value_block,
        preferred_element_type=jnp.float32,
    )
    summed = summed * jnp.transpose(fading, (2, 0, 1))[..., None] + product
    return (new_largest, totals, summed)


def keep_state(current):
    return current


def local(queries, keys, values, out_packed, out_scales, hadamard_signs):
    sequence_rows = queries.shape[0]
    my_index = lax.axis_index("blk")
    head_group = QUERY_HEADS // KEY_VALUE_HEADS
    query_positions = my_index * sequence_rows + jnp.arange(sequence_rows, dtype=jnp.int32)
    rows_of_queries = queries.reshape(sequence_rows, KEY_VALUE_HEADS, head_group, HEAD_SIZE)
    initial = (
        jnp.full((KEY_VALUE_HEADS, head_group, sequence_rows), masked_fill_value, jnp.float32),
        jnp.zeros((KEY_VALUE_HEADS, head_group, sequence_rows), jnp.float32),
        jnp.zeros((sequence_rows, KEY_VALUE_HEADS, head_group, HEAD_SIZE), jnp.float32),
    )
    last_position = jnp.max(query_positions)
    key_slice = lax.all_gather(keys, "blk", axis=0, tiled=True)
    value_slice = lax.all_gather(values, "blk", axis=0, tiled=True)
    block_count = key_slice.shape[0]
    width = math.gcd(block_count, 512)
    heads_of_keys = key_slice.reshape(block_count, KEY_VALUE_HEADS, HEAD_SIZE)
    heads_of_values = value_slice.reshape(block_count, KEY_VALUE_HEADS, HEAD_SIZE)

    def sweep(current):

        def one_step(turn, inner_state):
            begin = turn * width
            key_block = lax.dynamic_slice_in_dim(heads_of_keys, begin, width, 0)
            value_block = lax.dynamic_slice_in_dim(heads_of_values, begin, width, 0)
            key_positions = begin + jnp.arange(width, dtype=jnp.int32)
            return update(
                inner_state, rows_of_queries, query_positions, key_block, value_block, key_positions
            )

        return lax.fori_loop(0, block_count // width, one_step, current)

    final = lax.cond(jnp.int32(0) <= last_position, sweep, keep_state, initial)
    largest, totals, summed = final
    attention = (
        (summed / jnp.transpose(totals, (2, 0, 1))[..., None])
        .reshape(sequence_rows, QUERY_HEADS * HEAD_SIZE)
        .astype(jnp.bfloat16)
    )
    rotated = rotate(attention, hadamard_signs)
    weight = dequantize_rows(lax.all_gather(out_packed, "blk", axis=0, tiled=True), out_scales)
    mixed = jnp.dot(rotated, weight, preferred_element_type=jnp.float32)
    return mixed.astype(jnp.bfloat16)


def solution(mesh):
    in_specs = (
        P(("groups", "blk"), None),
        P(("groups", "blk"), None),
        P(("groups", "blk"), None),
        P("blk", None),
        P(),
        P(),
    )
    out_specs = P(("groups", "blk"), None)
    return jax.shard_map(local, mesh=mesh, in_specs=in_specs, out_specs=out_specs, check_vma=False)
```

profile of v0, /device:TPU:17, one launch (start us, length us, event | category | flops | bytes accessed | tf_op | source)
XLA Modules:
  0.0 238.7 jit_solution(12664698832807533376)
XLA Ops:
  6.5 1.7 copy.25
  8.3 1.7 copy.26
  12.6 38.3 %all-gather.4.cloned.1.call-done = bf16[2048,512]{0,1:T(8,128)(2,1)} async-done(((bf16[128,512]{0,1:T(8,128)(2,1)}), bf16[2048,512]{0,1:T(8,128)(2,1)}) %all-gather.4.cloned.1.call-update) | async-done | bytes 2097168 | tf_op jit(solution)/shard_map/all_gather | solution.py:97
  50.9 42.3 %all-gather.6.cloned.1.call-done = bf16[2048,512]{0,1:T(8,128)(2,1)} async-done(((bf16[128,512]{0,1:T(8,128)(2,1)}), bf16[2048,512]{0,1:T(8,128)(2,1)}) %all-gather.6.cloned.1.call-update) | async-done | bytes 2097168 | tf_op jit(solution)/shard_map/all_gather | solution.py:98
  93.2 69.7 %conditional.1 = (f32[4,8,128]{2,1,0:T(8,128)}, f32[128,4,8,128]{0,3,2,1:T(8,128)}) conditional(s32[]{:T(128)} %convert_element_type.53, () %tuple.27, (bf16[2048,512]{0,1:T(8,128)(2,1)}, bf16[2048,512]{0,1:T(8,128)(2,1)}, bf16[128,4096]{1,0:T(8,128)(2,1)}, s32[128]{0:T(128)S(1)}) %tuple.28), branch_computations={%region_1.0_spmd, %region_2.7_spmd} | conditional | flops 1098473984 | bytes 69735248 | solution.py:117
  93.2 1.6 copy.27
  95.5 67.4 %while.17 = (s32[]{:T(128)}, f32[4,8,128]{2,1,0:T(8,128)S(1)}, f32[4,8,128]{2,1,0:T(8,128)}, f32[128,4,8,128]{0,3,2,1:T(8,128)}, s32[128]{0:T(128)S(1)}, /*index...) while((s32[]{:T(128)}, f32[4,8,128]{2,1,0:T(8,128)S(1)}, ...), condition=%wide.region_6.6_spmd.clone, body=%wide.region_3.5_spmd.clone.sunk | while | flops 1098473984 | bytes 65540820 | solution.py:115
  95.7 5.7 %fusion.87 = (f32[4,8,128]{2,1,0:T(8,128)S(1)}, f32[4,512,128,8]{2,1,3,0:T(8,128)}) fusion(pred[128,512]{0,1:T(8,128)(4,1)S(1)} %broadcast_compare_fusion.2, bf16[128,4,8,128]{3,0,2,1:T(8,128)(2,1)S(1)} %get-tuple-element.326, bf16[2048,4,128]{0,2,1:T(8,128)(2,1)} %get-tuple-element.325, s32[]{:T(128)S(6)} %select_n.46), kind=kOutput, calls=%fused_computation.4.clone.1 | convolution fusion | flops 543158272 | bytes 10043396 | tf_op jit(solution)/shard_map/cond/branch_1_fun/while/body/eval_jaxpr/qkgd,nkd->kgqn/dot_general | solution.py:63
  101.5 7.8 %bitcast_add_fusion.2 = f32[128,4,8,128]{0,3,2,1:T(8,128)} fusion(f32[128,4,8,128]{0,3,2,1:T(8,128)} %get-tuple-element.311, f32[4,512,128,8]{2,1,3,0:T(8,128)} %get-tuple-element.294, f32[4,8,128]{2,1,0:T(8,128)S(1)} %get-tuple-element.321, pred[128,512]{0,1:T(8,128)(4,1)S(1)} %broadcast_compare_fusion.2, f32[128,4,8]{0,2,1:T(8,128)S(1)} %get-tuple-element.295, ...), kind=kOutput, calls=%fused_computation.10.clone.1 | convolution fusion | flops 546832384 | bytes 13205509 | tf_op jit(solution)/shard_map/cond/branch_1_fun/while/body/eval_jaxpr/kgqn,nkd->qkgd/dot_general | solution.py:71
  109.2 1.8 fusion.89
  111.8 5.7 %fusion.87 = (f32[4,8,128]{2,1,0:T(8,128)S(1)}, f32[4,512,128,8]{2,1,3,0:T(8,128)}) fusion(pred[128,512]{0,1:T(8,128)(4,1)S(1)} %broadcast_compare_fusion.2, bf16[128,4,8,128]{3,0,2,1:T(8,128)(2,1)S(1)} %get-tuple-element.326, bf16[2048,4,128]{0,2,1:T(8,128)(2,1)} %get-tuple-element.325, s32[]{:T(128)S(6)} %select_n.46), kind=kOutput, calls=%fused_computation.4.clone.1 | convolution fusion | flops 543158272 | bytes 10043396 | tf_op jit(solution)/shard_map/cond/branch_1_fun/while/body/eval_jaxpr/qkgd,nkd->kgqn/dot_general | solution.py:63
  117.6 7.9 %bitcast_add_fusion.2 = f32[128,4,8,128]{0,3,2,1:T(8,128)} fusion(f32[128,4,8,128]{0,3,2,1:T(8,128)} %get-tuple-element.311, f32[4,512,128,8]{2,1,3,0:T(8,128)} %get-tuple-element.294, f32[4,8,128]{2,1,0:T(8,128)S(1)} %get-tuple-element.321, pred[128,512]{0,1:T(8,128)(4,1)S(1)} %broadcast_compare_fusion.2, f32[128,4,8]{0,2,1:T(8,128)S(1)} %get-tuple-element.295, ...), kind=kOutput, calls=%fused_computation.10.clone.1 | convolution fusion | flops 546832384 | bytes 13205509 | tf_op jit(solution)/shard_map/cond/branch_1_fun/while/body/eval_jaxpr/kgqn,nkd->qkgd/dot_general | solution.py:71
  125.4 1.8 fusion.89
  127.2 1.3 fusion.90
  128.7 5.9 %fusion.87 = (f32[4,8,128]{2,1,0:T(8,128)S(1)}, f32[4,512,128,8]{2,1,3,0:T(8,128)}) fusion(pred[128,512]{0,1:T(8,128)(4,1)S(1)} %broadcast_compare_fusion.2, bf16[128,4,8,128]{3,0,2,1:T(8,128)(2,1)S(1)} %get-tuple-element.326, bf16[2048,4,128]{0,2,1:T(8,128)(2,1)} %get-tuple-element.325, s32[]{:T(128)S(6)} %select_n.46), kind=kOutput, calls=%fused_computation.4.clone.1 | convolution fusion | flops 543158272 | bytes 10043396 | tf_op jit(solution)/shard_map/cond/branch_1_fun/while/body/eval_jaxpr/qkgd,nkd->kgqn/dot_general | solution.py:63
  134.6 7.9 %bitcast_add_fusion.2 = f32[128,4,8,128]{0,3,2,1:T(8,128)} fusion(f32[128,4,8,128]{0,3,2,1:T(8,128)} %get-tuple-element.311, f32[4,512,128,8]{2,1,3,0:T(8,128)} %get-tuple-element.294, f32[4,8,128]{2,1,0:T(8,128)S(1)} %get-tuple-element.321, pred[128,512]{0,1:T(8,128)(4,1)S(1)} %broadcast_compare_fusion.2, f32[128,4,8]{0,2,1:T(8,128)S(1)} %get-tuple-element.295, ...), kind=kOutput, calls=%fused_computation.10.clone.1 | convolution fusion | flops 546832384 | bytes 13205509 | tf_op jit(solution)/shard_map/cond/branch_1_fun/while/body/eval_jaxpr/kgqn,nkd->qkgd/dot_general | solution.py:71
  142.5 1.8 fusion.89
  144.4 1.3 fusion.90
  145.9 5.7 %fusion.87 = (f32[4,8,128]{2,1,0:T(8,128)S(1)}, f32[4,512,128,8]{2,1,3,0:T(8,128)}) fusion(pred[128,512]{0,1:T(8,128)(4,1)S(1)} %broadcast_compare_fusion.2, bf16[128,4,8,128]{3,0,2,1:T(8,128)(2,1)S(1)} %get-tuple-element.326, bf16[2048,4,128]{0,2,1:T(8,128)(2,1)} %get-tuple-element.325, s32[]{:T(128)S(6)} %select_n.46), kind=kOutput, calls=%fused_computation.4.clone.1 | convolution fusion | flops 543158272 | bytes 10043396 | tf_op jit(solution)/shard_map/cond/branch_1_fun/while/body/eval_jaxpr/qkgd,nkd->kgqn/dot_general | solution.py:63
  151.6 8.2 %bitcast_add_fusion.2 = f32[128,4,8,128]{0,3,2,1:T(8,128)} fusion(f32[128,4,8,128]{0,3,2,1:T(8,128)} %get-tuple-element.311, f32[4,512,128,8]{2,1,3,0:T(8,128)} %get-tuple-element.294, f32[4,8,128]{2,1,0:T(8,128)S(1)} %get-tuple-element.321, pred[128,512]{0,1:T(8,128)(4,1)S(1)} %broadcast_compare_fusion.2, f32[128,4,8]{0,2,1:T(8,128)S(1)} %get-tuple-element.295, ...), kind=kOutput, calls=%fused_computation.10.clone.1 | convolution fusion | flops 546832384 | bytes 13205509 | tf_op jit(solution)/shard_map/cond/branch_1_fun/while/body/eval_jaxpr/kgqn,nkd->qkgd/dot_general | solution.py:71
  159.8 1.8 fusion.89
  162.9 1.8 divide_convert_fusion
  167.5 1.9 all-gather.8.cloned.1.call-done
  169.4 7.8 %and_dynamic-update-slice_fusion.7 = s32[4096,4096]{1,0:T(8,128)} fusion(s32[4096,512]{1,0:T(8,128)} %all-gather.8.cloned.1.call-done), kind=kLoop, calls=%fused_computation.37 | loop fusion | flops 4194303 | bytes 16777216
  177.2 4.3 %and_dynamic-update-slice_fusion.6 = s32[4096,4096]{1,0:T(8,128)} fusion(s32[4096,4096]{1,0:T(8,128)} %and_dynamic-update-slice_fusion.7, s32[4096,512]{1,0:T(8,128)S(1)} %copy-done.2), kind=kLoop, calls=%fused_computation.36 | loop fusion | flops 4194304 | bytes 16777216
  181.5 4.3 %and_dynamic-update-slice_fusion.5 = s32[4096,4096]{1,0:T(8,128)} fusion(s32[4096,4096]{1,0:T(8,128)} %and_dynamic-update-slice_fusion.6, s32[4096,512]{1,0:T(8,128)S(1)} %copy-done.2), kind=kLoop, calls=%fused_computation.35 | loop fusion | flops 4194304 | bytes 16777216
  185.7 4.2 %and_dynamic-update-slice_fusion.4 = s32[4096,4096]{1,0:T(8,128)} fusion(s32[4096,4096]{1,0:T(8,128)} %and_dynamic-update-slice_fusion.5, s32[4096,512]{1,0:T(8,128)S(1)} %copy-done.2), kind=kLoop, calls=%fused_computation.34 | loop fusion | flops 4194304 | bytes 16777216
  190.0 4.3 %and_dynamic-update-slice_fusion.3 = s32[4096,4096]{1,0:T(8,128)} fusion(s32[4096,4096]{1,0:T(8,128)} %and_dynamic-update-slice_fusion.4, s32[4096,512]{1,0:T(8,128)S(1)} %copy-done.2), kind=kLoop, calls=%fused_computation.33 | loop fusion | flops 4194304 | bytes 16777216
  194.2 4.2 %and_dynamic-update-slice_fusion.2 = s32[4096,4096]{1,0:T(8,128)} fusion(s32[4096,4096]{1,0:T(8,128)} %and_dynamic-update-slice_fusion.3, s32[4096,512]{1,0:T(8,128)S(1)} %copy-done.2), kind=kLoop, calls=%fused_computation.32 | loop fusion | flops 4194304 | bytes 16777216
  198.5 4.3 %and_dynamic-update-slice_fusion.1 = s32[4096,4096]{1,0:T(8,128)} fusion(s32[4096,4096]{1,0:T(8,128)} %and_dynamic-update-slice_fusion.2, s32[4096,512]{1,0:T(8,128)S(1)} %copy-done.2), kind=kLoop, calls=%fused_computation.31 | loop fusion | flops 4194304 | bytes 16777216
  202.8 4.3 %and_dynamic-update-slice_fusion = s32[4096,4096]{1,0:T(8,128)} fusion(s32[4096,4096]{1,0:T(8,128)} %and_dynamic-update-slice_fusion.1, s32[4096,512]{1,0:T(8,128)S(1)} %copy-done.2), kind=kLoop, calls=%fused_computation.30 | loop fusion | flops 4194304 | bytes 16777216 | tf_op jit(solution)/shard_map/concatenate | solution.py:57
  207.1 25.1 %fusion.23 = bf16[128,4096]{1,0:T(8,128)(2,1)} fusion(bf16[128,4096]{0,1:T(8,128)(2,1)S(1)} %bitcast.70, s32[4096,4096]{1,0:T(8,128)} %and_dynamic-update-slice_fusion, bf16[32,4096]{1,0:T(8,128)(2,1)S(1)} %copy-done, s32[4096]{0:T(1024)S(1)} %add_select_fusion), kind=kOutput, calls=%fused_computation.38 | convolution fusion | flops 5436473344 | bytes 69484544 | tf_op jit(solution)/shard_map/dot_general | solution.py:126
  (48 shorter events, 8.1 us)
Async XLA Ops:
  6.5 200.6 %copy-start = (bf16[32,4096]{1,0:T(8,128)(2,1)S(1)}, bf16[32,4096]{1,0:T(8,128)(2,1)}, u32[]{:S(2)}) copy-start(bf16[32,4096]{1,0:T(8,128)(2,1)} %param.14) | copy-start | bytes 786436
  6.5 44.4 %all-gather.4.cloned.1.call-start = ((), (), s32[]{:S(2)}) async-start(), calls=%async_computation | async-start | bytes 2228224 | tf_op jit(solution)/shard_map/all_gather | solution.py:97
  8.3 85.0 %all-gather.6.cloned.1.call-start = ((), (), s32[]{:S(2)}) async-start(), calls=%async_computation.1 | async-start | bytes 2228224 | tf_op jit(solution)/shard_map/all_gather | solution.py:98
  10.0 159.4 %all-gather.8.cloned.1.call-start = ((), (), s32[]{:S(2)}) async-start(), calls=%async_computation.2 | async-start | bytes 8912896 | tf_op jit(solution)/shard_map/all_gather | solution.py:125
  101.4 7.8 %copy-start.1 = (f32[4,512,128,8]{2,1,3,0:T(8,128)S(1)}, f32[4,512,128,8]{2,1,3,0:T(8,128)}, u32[]{:S(2)}) copy-start(f32[4,512,128,8]{2,1,3,0:T(8,128)} %get-tuple-element.294) | copy-start | bytes 25165828 | tf_op jit(solution)/shard_map/cond/branch_1_fun/while
  117.5 7.9 %copy-start.1 = (f32[4,512,128,8]{2,1,3,0:T(8,128)S(1)}, f32[4,512,128,8]{2,1,3,0:T(8,128)}, u32[]{:S(2)}) copy-start(f32[4,512,128,8]{2,1,3,0:T(8,128)} %get-tuple-element.294) | copy-start | bytes 25165828 | tf_op jit(solution)/shard_map/cond/branch_1_fun/while
  134.6 8.0 %copy-start.1 = (f32[4,512,128,8]{2,1,3,0:T(8,128)S(1)}, f32[4,512,128,8]{2,1,3,0:T(8,128)}, u32[]{:S(2)}) copy-start(f32[4,512,128,8]{2,1,3,0:T(8,128)} %get-tuple-element.294) | copy-start | bytes 25165828 | tf_op jit(solution)/shard_map/cond/branch_1_fun/while
  151.6 8.2 %copy-start.1 = (f32[4,512,128,8]{2,1,3,0:T(8,128)S(1)}, f32[4,512,128,8]{2,1,3,0:T(8,128)}, u32[]{:S(2)}) copy-start(f32[4,512,128,8]{2,1,3,0:T(8,128)} %get-tuple-element.294) | copy-start | bytes 25165828 | tf_op jit(solution)/shard_map/cond/branch_1_fun/while
  169.4 7.8 %copy-start.2 = (s32[4096,512]{1,0:T(8,128)S(1)}, s32[4096,512]{1,0:T(8,128)}, u32[]{:S(2)}) copy-start(s32[4096,512]{1,0:T(8,128)} %all-gather.8.cloned.1.call-done) | copy-start | bytes 25165828
Sparse Core Ops, SparseCore 0:
  9.5 41.3 all-gather.3
  53.1 40.1 all-gather.5
  95.4 73.9 all-gather.7
where the time goes:
time: 241 us; the launch traced here: 239 us
  waiting for transfers between devices  83.2 us (35%)
  matrix products  81.5 us (34%)
  other arithmetic  53.4 us (22%)
  between operations  13.7 us (6%)
  local copies, waits for them, and re-layouts  6.64 us (3%)
    all_gather x1, waiting for transfers between devices, local(): value_slice = lax.all_gather(values, 'blk', axis=0, tiled=True)  42.3 us
    all_gather x1, waiting for transfers between devices, local(): key_slice = lax.all_gather(keys, 'blk', axis=0, tiled=True)  38.3 us
    unnamed x7, other arithmetic  33.4 us
    dot_general x4, matrix products, update(): jnp.einsum('kgqn,nkd->qkgd', weights.astype(jnp.bfloat16), value_block, p...  31.7 us
    dot_general x1, matrix products, local(): mixed = jnp.dot(rotated, weight, preferred_element_type=jnp.float32)  25.1 us
    dot_general x4, matrix products, update(): jnp.einsum('qkgd,nkd->kgqn', query_tile, key_block, preferred_element_typ...  23 us
    reduce_sum x4, other arithmetic, update(): totals = totals * fading + jnp.sum(weights, axis=-1)  7.23 us
  transfers between devices with their start and end apart: 3, of which 3 were waited for; matrix products, arithmetic and copies ran while one was open for 32% of the time, Pallas kernels for 0%

commit v1 on v0

v1 whole, which is shorter than its diff:
```python
import functools
import math

import jax
import jax.numpy as jnp
from jax import lax
from jax.experimental import pallas as pl
from jax.experimental.pallas import tpu as pltpu
from jax.sharding import PartitionSpec as P

HEAD_SIZE = 128
QUERY_HEADS = 32
KEY_VALUE_HEADS = 4
GROUP = 128
HEAD_GROUP = QUERY_HEADS // KEY_VALUE_HEADS
NEGATIVE = -1e30
EXPONENT = math.log2(math.e) / math.sqrt(HEAD_SIZE)
MESH = pl.DeviceIdType.MESH


def sylvester(block_count):
    index = jnp.arange(block_count, dtype=jnp.int32)
    both = jnp.bitwise_and(index[:, None], index[None, :])
    parity = jnp.zeros((block_count, block_count), jnp.int32)
    for bit_number in range(block_count.bit_length() - 1):
        parity = jnp.bitwise_xor(parity, jnp.bitwise_and(jnp.right_shift(both, bit_number), 1))
    return (1 - 2 * parity).astype(jnp.bfloat16)


def kernel(
    n, groups, share, early,
    q_ref, kv_ref, packed_ref, scales_ref, signs_ref, table_ref, out_ref,
    kv_all, packed_all, qs, acc, largest, totals, inner, rotated, weight,
    local_sem, kv_send, kv_recv, kv_psend, kv_precv, p_send, p_recv, p_psend, p_precv,
    x_send, x_recv, x_psend, x_precv,
):
    rows = q_ref.shape[0]
    half_rows = rows // 2
    packed_rows = packed_ref.shape[0]
    words = packed_ref.shape[1]
    share_rows = packed_rows // share
    seg = share_rows // 2
    chips = n // 2
    kv_width = KEY_VALUE_HEADS * HEAD_SIZE

    me = lax.axis_index("blk")
    my_group = lax.axis_index("groups")
    core = lax.rem(me, 2)
    partner = me + 1 - 2 * core
    chip = me // 2
    pos = jnp.where(lax.rem(chip, 2) == 0, chip // 2, chips - 1 - chip // 2)

    def chip_at(place):
        place = lax.rem(place + chips, chips)
        return jnp.where(place < chips // 2, 2 * place, 2 * (chips - 1 - place) + 1)

    after = chip_at(pos + 1) * 2 + core
    before = chip_at(pos - 1) * 2 + core
    ring_to = (after, before)
    my_share = my_group if share > 1 else jnp.int32(0)

    barrier = pltpu.get_barrier_semaphore()
    for target in (after, before, partner):
        pl.semaphore_signal(barrier, inc=1, device_id={"blk": target}, device_id_type=MESH)
    for j in range(1, share):
        pl.semaphore_signal(
            barrier, inc=1, device_id={"groups": lax.rem(my_group + j, groups)}, device_id_type=MESH
        )
    pl.semaphore_wait(barrier, 3 + share - 1)

    def owner_chip(d, s):
        return chip_at(pos - s) if d == 0 else chip_at(pos + s)

    def kv_rows(owner, d):
        return pl.ds(pl.multiple_of(owner * rows + d * half_rows, half_rows), half_rows)

    def p_rows(owner, piece, d):
        return pl.ds(
            pl.multiple_of(owner * packed_rows + piece * share_rows + d * seg, seg), seg
        )

    def remote(src, dst, send, recv, device):
        return pltpu.make_async_remote_copy(
            src_ref=src, dst_ref=dst, send_sem=send, recv_sem=recv,
            device_id=device, device_id_type=MESH,
        )

    def kv_ring(d, s):
        where = kv_all.at[kv_rows(owner_chip(d, s) * 2 + core, d)]
        return remote(where, where, kv_send.at[d, s], kv_recv.at[d, s + 1], {"blk": ring_to[d]})

    def kv_relay(d, s):
        where = kv_all.at[kv_rows(owner_chip(d, s) * 2 + core, d)]
        return remote(where, where, kv_psend.at[d, s], kv_precv.at[d, s], {"blk": partner})

    def p_ring(d, s):
        where = packed_all.at[p_rows(owner_chip(d, s) * 2 + core, my_share, d)]
        return remote(where, where, p_send.at[d, s], p_recv.at[d, s + 1], {"blk": ring_to[d]})

    def p_relay(d, s):
        where = packed_all.at[p_rows(owner_chip(d, s) * 2 + core, my_share, d)]
        return remote(where, where, p_psend.at[d, s], p_precv.at[d, s], {"blk": partner})

    def x_copy(j, d, s):
        where = packed_all.at[p_rows(owner_chip(d, s) * 2 + core, my_share, d)]
        return remote(
            where, where, x_send.at[j - 1, d, s], x_recv.at[j - 1, d, s],
            {"groups": lax.rem(my_group + j, groups)},
        )

    def x_relay(j, d, s):
        piece = lax.rem(my_group - j + groups, groups)
        where = packed_all.at[p_rows(owner_chip(d, s) * 2 + core, piece, d)]
        return remote(
            where, where, x_psend.at[j - 1, d, s], x_precv.at[j - 1, d, s], {"blk": partner}
        )

    own_kv = kv_all.at[pl.ds(pl.multiple_of(me * rows, rows), rows)]
    own_packed = packed_all.at[pl.ds(pl.multiple_of(me * packed_rows, packed_rows), packed_rows)]
    kv_local = pltpu.make_async_copy(kv_ref, own_kv, local_sem.at[0])
    p_local = pltpu.make_async_copy(packed_ref, own_packed, local_sem.at[1])
    kv_own = remote(kv_ref, own_kv, kv_psend.at[0, 0], kv_precv.at[0, 0], {"blk": partner})
    p_own = remote(packed_ref, own_packed, p_psend.at[0, 0], p_precv.at[0, 0], {"blk": partner})
    kv_local.start()
    p_local.start()
    kv_local.wait()
    kv_own.start()
    for d in (0, 1):
        kv_ring(d, 0).start()
    p_local.wait()
    for d in (0, 1):
        p_ring(d, 0).start()
    p_own.start()

    for h in range(QUERY_HEADS):
        g, r = divmod(h, HEAD_GROUP)
        qs[g, r * rows:(r + 1) * rows, :] = q_ref[:, h * HEAD_SIZE:(h + 1) * HEAD_SIZE]

    def attend(pieces, bias, first):
        tile = 2 * rows
        for g in range(KEY_VALUE_HEADS):
            k = jnp.concatenate(
                [kv_all[p, g * HEAD_SIZE:(g + 1) * HEAD_SIZE] for p in pieces], axis=0
            )
            v = jnp.concatenate(
                [kv_all[p, kv_width + g * HEAD_SIZE:kv_width + (g + 1) * HEAD_SIZE] for p in pieces],
                axis=0,
            )
            vt = v.T
            for c in range(HEAD_GROUP * rows // tile):
                cols = slice(c * tile, (c + 1) * tile)
                scores = lax.dot_general(
                    k, qs[g, cols, :], (((1,), (1,)), ((), ())), preferred_element_type=jnp.float32
                )
                scores = scores + bias
                top = jnp.max(scores, axis=0, keepdims=True)
                if not first:
                    old = largest[g, :, cols]
                    top = jnp.maximum(old, top)
                    fading = jnp.exp2((old - top) * EXPONENT)
                weights = jnp.exp2((scores - top) * EXPONENT)
                total = jnp.sum(weights, axis=0, keepdims=True)
                product = jnp.dot(
                    vt, weights.astype(jnp.bfloat16), preferred_element_type=jnp.float32
                )
                if first:
                    totals[g, :, cols] = total
                    acc[g, :, cols] = product
                else:
                    totals[g, :, cols] = totals[g, :, cols] * fading + total
                    acc[g, :, cols] = acc[g, :, cols] * fading + product
                largest[g, :, cols] = top

    chunk = math.gcd(seg, 32)

    def dequantize(row, target):
        base = packed_all[pl.ds(pl.multiple_of(row, chunk), chunk), :]
        flipped = jnp.bitwise_xor(base, jnp.int32(-2004318072))
        scale_index = row // GROUP
        for nibble in range(8):
            level = jnp.right_shift(jnp.left_shift(flipped, 28 - 4 * nibble), 28)
            scale = scales_ref[pl.ds(scale_index, 1), nibble * words:(nibble + 1) * words]
            weight[pl.ds(pl.multiple_of(target, chunk), chunk), nibble * words:(nibble + 1) * words] = (
                level.astype(jnp.float32) * scale
            ).astype(jnp.bfloat16)

    def dequantize_rows(first_row, count):
        @pl.loop(0, count // chunk)
        def _(t):
            dequantize(first_row + t * chunk, first_row + t * chunk)

    kv_own.wait_recv()
    key_pos = chip * 2 * rows + lax.broadcasted_iota(jnp.int32, (2 * rows, 2 * rows), 0)
    query_pos = me * rows + lax.rem(lax.broadcasted_iota(jnp.int32, (2 * rows, 2 * rows), 1), rows)
    attend(
        [pl.ds(pl.multiple_of(chip * 2 * rows, 2 * rows), 2 * rows)],
        jnp.where(key_pos <= query_pos, 0.0, NEGATIVE),
        True,
    )
    p_own.wait_recv()
    if early:
        dequantize_rows(chip * 2 * packed_rows, 2 * packed_rows)

    def finish_packed(s):
        for d in (0, 1):
            for j in range(1, share):
                x_copy(j, d, s).wait_recv()
                x_relay(j, d, s).start()
        for d in (0, 1):
            p_relay(d, s).wait_recv()
        def pieces(t):
            owner_core = lax.rem(t, 2)
            piece = t // 2
            for d in (0, 1):
                owner = owner_chip(d, s) * 2 + owner_core
                dequantize_rows(owner * packed_rows + piece * share_rows + d * seg, seg)
        for d in (0, 1):
            for j in range(1, share):
                x_relay(j, d, s).wait_recv()
        if early:
            pl.loop(0, 2 * share)(pieces)

    @pl.loop(1, chips)
    def _(s):
        for d in (0, 1):
            kv_ring(d, s - 1).wait_recv()

            @pl.when(s < chips - 1)
            def _():
                kv_ring(d, s).start()

            kv_relay(d, s).start()
        for d in (0, 1):
            p_ring(d, s - 1).wait_recv()

            @pl.when(s < chips - 1)
            def _():
                p_ring(d, s).start()

            for j in range(1, share):
                x_copy(j, d, s).start()
            p_relay(d, s).start()
        for d in (0, 1):
            kv_relay(d, s).wait_recv()
        first_chip, second_chip = owner_chip(0, s), owner_chip(1, s)

        @pl.when((first_chip < chip) | (second_chip < chip))
        def _():
            key_row = lax.broadcasted_iota(jnp.int32, (2 * rows, 1), 0)
            needed = jnp.where(key_row < rows, (first_chip < chip).astype(jnp.int32), (second_chip < chip).astype(jnp.int32))
            bias = jnp.where(needed > 0, 0.0, NEGATIVE)
            attend(
                [
                    kv_rows(first_chip * 2, 0), kv_rows(first_chip * 2 + 1, 0),
                    kv_rows(second_chip * 2, 1), kv_rows(second_chip * 2 + 1, 1),
                ],
                bias, False,
            )

        @pl.when(s > 1)
        def _():
            finish_packed(s - 1)

    for g in range(KEY_VALUE_HEADS):
        for r in range(HEAD_GROUP):
            h = g * HEAD_GROUP + r
            cols = slice(r * rows, (r + 1) * rows)
            attention = (acc[g, :, cols] / totals[g, :, cols]).T.astype(jnp.bfloat16)
            signed = attention * signs_ref[:, h * HEAD_SIZE:(h + 1) * HEAD_SIZE]
            inner[h] = jnp.dot(signed, table_ref[...], preferred_element_type=jnp.float32)

    @pl.loop(0, rows // 16)
    def _(t):
        these = pl.ds(pl.multiple_of(t * 16, 16), 16)
        heads = [inner[h, these, :] for h in range(QUERY_HEADS)]
        step = 1
        while step < QUERY_HEADS:
            done = list(heads)
            for h in range(QUERY_HEADS):
                if h & step == 0:
                    done[h] = heads[h] + heads[h + step]
                    done[h + step] = heads[h] - heads[h + step]
            heads = done
            step *= 2
        for h in range(QUERY_HEADS):
            rotated[these, h * HEAD_SIZE:(h + 1) * HEAD_SIZE] = (
                heads[h] * (1.0 / math.sqrt(QUERY_HEADS * HEAD_SIZE))
            ).astype(jnp.bfloat16)

    finish_packed(chips - 1)

    depth = n * packed_rows
    out_width = out_ref.shape[1]
    if early:
        tile = 512

        @pl.loop(0, out_width // tile)
        def _(t):
            cols = pl.ds(pl.multiple_of(t * tile, tile), tile)
            out_ref[:, cols] = jnp.dot(
                rotated[...], weight[:, cols], preferred_element_type=jnp.float32
            ).astype(jnp.bfloat16)
    else:
        span = weight.shape[0]
        tile = HEAD_GROUP * rows
        acc[...] = jnp.zeros_like(acc)

        @pl.loop(0, depth // span)
        def _(k):
            @pl.loop(0, span // chunk)
            def _(t):
                dequantize(k * span + t * chunk, t * chunk)

            left = rotated[:, pl.ds(pl.multiple_of(k * span, span), span)]
            for c in range(KEY_VALUE_HEADS):
                acc[c] += jnp.dot(
                    left, weight[:, c * tile:(c + 1) * tile], preferred_element_type=jnp.float32
                )

        for c in range(KEY_VALUE_HEADS):
            out_ref[:, c * tile:(c + 1) * tile] = acc[c].astype(jnp.bfloat16)

    kv_own.wait_send()
    p_own.wait_send()
    for d in (0, 1):
        kv_ring(d, 0).wait_send()
        p_ring(d, 0).wait_send()

    @pl.loop(1, chips)
    def _(s):
        for d in (0, 1):
            @pl.when(s < chips - 1)
            def _():
                kv_ring(d, s).wait_send()
                p_ring(d, s).wait_send()

            kv_relay(d, s).wait_send()
            p_relay(d, s).wait_send()
            for j in range(1, share):
                x_copy(j, d, s).wait_send()
                x_relay(j, d, s).wait_send()


def local(n, groups, queries, keys, values, out_packed, out_scales, hadamard_signs):
    rows = queries.shape[0]
    packed_rows, words = out_packed.shape
    width = queries.shape[1]
    share = groups if packed_rows % (32 * groups) == 0 else 1
    chips = n // 2
    kv = jnp.concatenate([keys, values], axis=1)
    scales = out_scales.astype(jnp.float32)
    signs = (2 * hadamard_signs - 1).astype(jnp.bfloat16).reshape(1, width)
    depth = n * packed_rows
    out_width = 8 * words
    kv_bytes = n * rows * kv.shape[1] * 2
    early = kv_bytes + depth * out_width * 2 + depth * words * 4 < 46 * 2**20
    others = max(share - 1, 1)
    dma = pltpu.SemaphoreType.DMA
    spec = pl.BlockSpec(memory_space=pltpu.VMEM)
    return pl.pallas_call(
        functools.partial(kernel, n, groups, share, early),
        out_shape=jax.ShapeDtypeStruct((rows, out_width), jnp.bfloat16),
        in_specs=[spec] * 6,
        out_specs=spec,
        scratch_shapes=[
            pltpu.VMEM((n * rows, kv.shape[1]), jnp.bfloat16),
            pltpu.VMEM((depth, words), jnp.int32),
            pltpu.VMEM((KEY_VALUE_HEADS, HEAD_GROUP * rows, HEAD_SIZE), jnp.bfloat16),
            pltpu.VMEM((KEY_VALUE_HEADS, HEAD_SIZE, HEAD_GROUP * rows), jnp.float32),
            pltpu.VMEM((KEY_VALUE_HEADS, 1, HEAD_GROUP * rows), jnp.float32),
            pltpu.VMEM((KEY_VALUE_HEADS, 1, HEAD_GROUP * rows), jnp.float32),
            pltpu.VMEM((QUERY_HEADS, rows, HEAD_SIZE), jnp.float32),
            pltpu.VMEM((rows, width), jnp.bfloat16),
            pltpu.VMEM((depth if early else 256, out_width), jnp.bfloat16),
            dma((2,)),
        ]
        + [dma((2, chips))] * 8
        + [dma((others, 2, chips))] * 4,
        compiler_params=pltpu.CompilerParams(
            collective_id=0, has_side_effects=True, vmem_limit_bytes=64000000
        ),
    )(queries, kv, out_packed, scales, signs, sylvester(HEAD_SIZE))


def solution(mesh):
    in_specs = (
        P(("groups", "blk"), None),
        P(("groups", "blk"), None),
        P(("groups", "blk"), None),
        P("blk", None),
        P(),
        P(),
    )
    out_specs = P(("groups", "blk"), None)
    body = functools.partial(local, mesh.shape["blk"], mesh.shape["groups"])
    return jax.shard_map(body, mesh=mesh, in_specs=in_specs, out_specs=out_specs, check_vma=False)
```

time: 241 us -> 88.8 us (0.37)
  waiting for transfers between devices: 83.2 us -> 0 us
  Pallas kernels: 0 us -> 81.7 us
  matrix products: 81.5 us -> 0 us
  other arithmetic: 53.4 us -> 3.96 us
  between operations: 13.7 us -> 0.01 us
  local copies, waits for them, and re-layouts: 6.64 us -> 2.9 us
    all_gather x3 -> x0, waiting for transfers between devices: 82.4 us -> none  [the longest x1 42.3 us: local(): value_slice = lax.all_gather(values, 'blk', axis=0, tiled=True)]
    pallas_call x0 -> x1, Pallas kernels: none -> 81.7 us  [local(): pl.pallas_call(functools.partial(kernel, n, groups, share, early), out_sh...]
    dot_general x12 -> x0, matrix products: 81.5 us -> none  [the longest x4 31.7 us: update(): jnp.einsum('kgqn,nkd->qkgd', weights.astype(jnp.bfloat16), value_block, p...]
    unnamed x7 -> x0, other arithmetic: 33.4 us -> none
    reduce_sum x4 -> x0, other arithmetic: 7.23 us -> none  [update(): totals = totals * fading + jnp.sum(weights, axis=-1)]
    add x9 -> x0, other arithmetic: 4.69 us -> none  [the longest x4 4.67 us: update(): totals = totals * fading + jnp.sum(weights, axis=-1)]
    concatenate x1, other arithmetic: 4.31 us -> 1.74 us  [local(): kv = jnp.concatenate([keys, values], axis=1)]
  transfers between devices with their start and end apart: 3 -> 0, of which waited for: 3 -> 0; matrix products, arithmetic and copies ran while one was open for 32% -> 0% of each run, Pallas kernels for 0% -> 0%
where the time goes in v1:
time: 88.8 us; the launch traced here: 88.6 us
  Pallas kernels  81.7 us (92%)
  other arithmetic  3.96 us (4%)
  local copies, waits for them, and re-layouts  2.9 us (3%)
    pallas_call x1, Pallas kernels, local(): pl.pallas_call(functools.partial(kernel, n, groups, share, early), out_sh...  81.7 us
    unnamed x3, local copies, waits for them, and re-layouts  2.29 us

profile of v1, /device:TPU:17, one launch (start us, length us, event | category | flops | bytes accessed | tf_op | source)
XLA Modules:
  0.0 88.6 jit_solution(6665871662351787848)
XLA Ops:
  0.0 0.7 add_convert_fusion
  0.7 0.6 reshape.3.signs_ref
  1.3 0.7 subtract_convert_fusion.table_ref
  2.0 0.0 copy-start
  2.0 1.7 %pad_maximum_fusion.kv_ref = bf16[128,1024]{1,0:T(8,128)(2,1)} fusion(bf16[128,512]{1,0:T(8,128)(2,1)} %param.8, bf16[128,512]{1,0:T(8,128)(2,1)} %param.7), kind=kLoop, calls=%fused_computation | loop fusion | flops 524288 | bytes 524288 | tf_op jit(solution)/shard_map/concatenate | solution.py:350
  3.7 0.0 copy-done
  3.7 0.8 convert_element_type.9.scales_ref
  4.6 81.7 %shard_map.64 = bf16[128,4096]{1,0:T(8,128)(2,1)} custom-call(bf16[128,4096]{1,0:T(8,128)(2,1)} %q_ref.1, bf16[128,1024]{1,0:T(8,128)(2,1)} %pad_maximum_fusion.kv_ref, s32[256,512]{1,0:T(8,128)} %packed_ref.1, f32[32,4096]{1,0:T(8,128)} %convert_element_type.9.scales_ref, bf16[1,4096]{1,0:T(2,128)(2,1)} %reshape.3.signs_ref, ...), custom_call_target="tpu_custom_call" | custom-call | tf_op jit(solution)/shard_map/pallas_call | solution.py:360
  86.3 2.3 %copy.8 = bf16[128,4096]{1,0:T(8,128)(2,1)} copy(bf16[128,4096]{1,0:T(8,128)(2,1)} %shard_map.64) | data formatting | bytes 2097152
Async XLA Ops:
  2.0 1.7 %copy-start = (bf16[32,4096]{1,0:T(8,128)(2,1)S(1)}, bf16[32,4096]{1,0:T(8,128)(2,1)}, u32[]{:S(2)}) copy-start(bf16[32,4096]{1,0:T(8,128)(2,1)} %param.10) | copy-start | bytes 786436

commit v2 on v1

--- a/solution.py
+++ b/solution.py
@@ -18,19 +18,10 @@
 MESH = pl.DeviceIdType.MESH
 
 
-def sylvester(block_count):
-    index = jnp.arange(block_count, dtype=jnp.int32)
-    both = jnp.bitwise_and(index[:, None], index[None, :])
-    parity = jnp.zeros((block_count, block_count), jnp.int32)
-    for bit_number in range(block_count.bit_length() - 1):
-        parity = jnp.bitwise_xor(parity, jnp.bitwise_and(jnp.right_shift(both, bit_number), 1))
-    return (1 - 2 * parity).astype(jnp.bfloat16)
-
-
 def kernel(
     n, groups, share, early,
-    q_ref, kv_ref, packed_ref, scales_ref, signs_ref, table_ref, out_ref,
-    kv_all, packed_all, qs, acc, largest, totals, inner, rotated, weight,
+    q_ref, k_ref, v_ref, packed_ref, scales_ref, signs_ref, out_ref,
+    kv_all, packed_all, qs, acc, largest, totals, inner, rotated, weight, scales,
     local_sem, kv_send, kv_recv, kv_psend, kv_precv, p_send, p_recv, p_psend, p_precv,
     x_send, x_recv, x_psend, x_precv,
 ):
@@ -117,16 +108,24 @@
 
     own_kv = kv_all.at[pl.ds(pl.multiple_of(me * rows, rows), rows)]
     own_packed = packed_all.at[pl.ds(pl.multiple_of(me * packed_rows, packed_rows), packed_rows)]
-    kv_local = pltpu.make_async_copy(kv_ref, own_kv, local_sem.at[0])
+    own_rows = pl.ds(pl.multiple_of(me * rows, rows), rows)
+    k_local = pltpu.make_async_copy(
+        k_ref, kv_all.at[own_rows, pl.ds(0, kv_width)], local_sem.at[0]
+    )
+    v_local = pltpu.make_async_copy(
+        v_ref, kv_all.at[own_rows, pl.ds(kv_width, kv_width)], local_sem.at[2]
+    )
     p_local = pltpu.make_async_copy(packed_ref, own_packed, local_sem.at[1])
-    kv_own = remote(kv_ref, own_kv, kv_psend.at[0, 0], kv_precv.at[0, 0], {"blk": partner})
+    kv_own = remote(own_kv, own_kv, kv_psend.at[0, 0], kv_precv.at[0, 0], {"blk": partner})
     p_own = remote(packed_ref, own_packed, p_psend.at[0, 0], p_precv.at[0, 0], {"blk": partner})
-    kv_local.start()
+    k_local.start()
+    v_local.start()
     p_local.start()
-    kv_local.wait()
-    kv_own.start()
+    k_local.wait()
+    v_local.wait()
     for d in (0, 1):
         kv_ring(d, 0).start()
+    kv_own.start()
     p_local.wait()
     for d in (0, 1):
         p_ring(d, 0).start()
@@ -135,6 +134,8 @@
     for h in range(QUERY_HEADS):
         g, r = divmod(h, HEAD_GROUP)
         qs[g, r * rows:(r + 1) * rows, :] = q_ref[:, h * HEAD_SIZE:(h + 1) * HEAD_SIZE]
+
+    scales[...] = scales_ref[...].astype(jnp.float32)
 
     def attend(pieces, bias, first):
         tile = 2 * rows
@@ -179,7 +180,7 @@
         scale_index = row // GROUP
         for nibble in range(8):
             level = jnp.right_shift(jnp.left_shift(flipped, 28 - 4 * nibble), 28)
-            scale = scales_ref[pl.ds(scale_index, 1), nibble * words:(nibble + 1) * words]
+            scale = scales[pl.ds(scale_index, 1), nibble * words:(nibble + 1) * words]
             weight[pl.ds(pl.multiple_of(target, chunk), chunk), nibble * words:(nibble + 1) * words] = (
                 level.astype(jnp.float32) * scale
             ).astype(jnp.bfloat16)
@@ -197,28 +198,33 @@
         jnp.where(key_pos <= query_pos, 0.0, NEGATIVE),
         True,
     )
-    p_own.wait_recv()
-    if early:
-        dequantize_rows(chip * 2 * packed_rows, 2 * packed_rows)
-
-    def finish_packed(s):
-        for d in (0, 1):
-            for j in range(1, share):
-                x_copy(j, d, s).wait_recv()
-                x_relay(j, d, s).start()
-        for d in (0, 1):
-            p_relay(d, s).wait_recv()
-        def pieces(t):
-            owner_core = lax.rem(t, 2)
-            piece = t // 2
+
+    def dequantize_piece(piece, s):
+        @pl.loop(0, 2)
+        def _(owner_core):
             for d in (0, 1):
                 owner = owner_chip(d, s) * 2 + owner_core
                 dequantize_rows(owner * packed_rows + piece * share_rows + d * seg, seg)
+
+    def take_ring(s):
+        for d in (0, 1):
+            p_relay(d, s).wait_recv()
+        if early:
+            dequantize_piece(my_share, s)
+
+    def start_relay(s):
+        for d in (0, 1):
+            for j in range(1, share):
+                x_copy(j, d, s).wait_recv()
+                x_relay(j, d, s).start()
+
+    def take_other(s):
         for d in (0, 1):
             for j in range(1, share):
                 x_relay(j, d, s).wait_recv()
         if early:
-            pl.loop(0, 2 * share)(pieces)
+            for j in range(1, share):
+                dequantize_piece(lax.rem(my_group - j + groups, groups), s)
 
     @pl.loop(1, chips)
     def _(s):
@@ -230,6 +236,21 @@
                 kv_ring(d, s).start()
 
             kv_relay(d, s).start()
+
+        @pl.when(s == 1)
+        def _():
+            p_own.wait_recv()
+            if early:
+                dequantize_rows(chip * 2 * packed_rows, 2 * packed_rows)
+
+        @pl.when(s > 1)
+        def _():
+            take_ring(s - 1)
+
+        @pl.when(s > 2)
+        def _():
+            take_other(s - 2)
+
         for d in (0, 1):
             p_ring(d, s - 1).wait_recv()
 
@@ -259,15 +280,34 @@
 
         @pl.when(s > 1)
         def _():
-            finish_packed(s - 1)
-
+            start_relay(s - 1)
+
+    tail = early and share > 1 and 2 * seg == HEAD_SIZE
+    take_ring(chips - 1)
+    if chips > 2:
+        take_other(chips - 2)
+    if tail:
+        for owner_core in (0, 1):
+            for j in range(1, share):
+                piece = lax.rem(my_group - j + groups, groups)
+                for d in (0, 1):
+                    owner = owner_chip(d, chips - 1) * 2 + owner_core
+                    weight[p_rows(owner, piece, d), :] = jnp.zeros((seg, weight.shape[1]), jnp.bfloat16)
+
+    index = lax.broadcasted_iota(jnp.int32, (HEAD_SIZE, HEAD_SIZE), 0)
+    both = jnp.bitwise_and(index, lax.broadcasted_iota(jnp.int32, (HEAD_SIZE, HEAD_SIZE), 1))
+    parity = jnp.zeros_like(both)
+    for bit_number in range(HEAD_SIZE.bit_length() - 1):
+        parity = jnp.bitwise_xor(parity, jnp.bitwise_and(jnp.right_shift(both, bit_number), 1))
+    table = (1 - 2 * parity).astype(jnp.float32).astype(jnp.bfloat16)
     for g in range(KEY_VALUE_HEADS):
         for r in range(HEAD_GROUP):
             h = g * HEAD_GROUP + r
             cols = slice(r * rows, (r + 1) * rows)
             attention = (acc[g, :, cols] / totals[g, :, cols]).T.astype(jnp.bfloat16)
-            signed = attention * signs_ref[:, h * HEAD_SIZE:(h + 1) * HEAD_SIZE]
-            inner[h] = jnp.dot(signed, table_ref[...], preferred_element_type=jnp.float32)
+            sign = (2 * signs_ref[h:h + 1, :] - 1).astype(jnp.float32).astype(jnp.bfloat16)
+            signed = attention * sign
+            inner[h] = jnp.dot(signed, table, preferred_element_type=jnp.float32)
 
     @pl.loop(0, rows // 16)
     def _(t):
@@ -287,20 +327,52 @@
                 heads[h] * (1.0 / math.sqrt(QUERY_HEADS * HEAD_SIZE))
             ).astype(jnp.bfloat16)
 
-    finish_packed(chips - 1)
-
     depth = n * packed_rows
     out_width = out_ref.shape[1]
-    if early:
-        tile = 512
-
+    tile = HEAD_GROUP * rows if tail else 512
+    if tail:
+        for c in range(out_width // tile):
+            @pl.loop(0, tile // 512)
+            def _(t):
+                acc[c, :, pl.ds(pl.multiple_of(t * 512, 512), 512)] = jnp.dot(
+                    rotated[...],
+                    weight[:, pl.ds(pl.multiple_of(c * tile + t * 512, 512), 512)],
+                    preferred_element_type=jnp.float32,
+                )
+
+        start_relay(chips - 1)
+        take_other(chips - 1)
+        lane = lax.broadcasted_iota(jnp.int32, (rows, HEAD_SIZE), 1)
+        left = []
+        right = []
+        for owner_core in (0, 1):
+            for j in range(1, share):
+                piece = lax.rem(my_group - j + groups, groups)
+                for d in (0, 1):
+                    owner = owner_chip(d, chips - 1) * 2 + owner_core
+                    begin = pl.multiple_of(owner * packed_rows + piece * share_rows, HEAD_SIZE)
+                    part = rotated[:, pl.ds(begin, HEAD_SIZE)].astype(jnp.float32)
+                    left.append(jnp.where(lane // seg == d, part, 0.0).astype(jnp.bfloat16))
+                    right.append(pl.ds(begin, HEAD_SIZE))
+        for c in range(out_width // 512):
+            g, r = divmod(c * 512, tile)
+            total = acc[g, :, r:r + 512]
+            for part, where in zip(left, right):
+                total = total + jnp.dot(
+                    part, weight[where, c * 512:(c + 1) * 512], preferred_element_type=jnp.float32
+                )
+            out_ref[:, c * 512:(c + 1) * 512] = total.astype(jnp.bfloat16)
+    else:
+        start_relay(chips - 1)
+        take_other(chips - 1)
+    if early and not tail:
         @pl.loop(0, out_width // tile)
         def _(t):
             cols = pl.ds(pl.multiple_of(t * tile, tile), tile)
             out_ref[:, cols] = jnp.dot(
                 rotated[...], weight[:, cols], preferred_element_type=jnp.float32
             ).astype(jnp.bfloat16)
-    else:
+    elif not early:
         span = weight.shape[0]
         tile = HEAD_GROUP * rows
         acc[...] = jnp.zeros_like(acc)
@@ -347,12 +419,11 @@
     width = queries.shape[1]
     share = groups if packed_rows % (32 * groups) == 0 else 1
     chips = n // 2
-    kv = jnp.concatenate([keys, values], axis=1)
-    scales = out_scales.astype(jnp.float32)
-    signs = (2 * hadamard_signs - 1).astype(jnp.bfloat16).reshape(1, width)
+    kv_columns = 2 * keys.shape[1]
+    signs = hadamard_signs.reshape(QUERY_HEADS, HEAD_SIZE)
     depth = n * packed_rows
     out_width = 8 * words
-    kv_bytes = n * rows * kv.shape[1] * 2
+    kv_bytes = n * rows * kv_columns * 2
     early = kv_bytes + depth * out_width * 2 + depth * words * 4 < 46 * 2**20
     others = max(share - 1, 1)
     dma = pltpu.SemaphoreType.DMA
@@ -363,7 +434,7 @@
         in_specs=[spec] * 6,
         out_specs=spec,
         scratch_shapes=[
-            pltpu.VMEM((n * rows, kv.shape[1]), jnp.bfloat16),
+            pltpu.VMEM((n * rows, kv_columns), jnp.bfloat16),
             pltpu.VMEM((depth, words), jnp.int32),
             pltpu.VMEM((KEY_VALUE_HEADS, HEAD_GROUP * rows, HEAD_SIZE), jnp.bfloat16),
             pltpu.VMEM((KEY_VALUE_HEADS, HEAD_SIZE, HEAD_GROUP * rows), jnp.float32),
@@ -372,14 +443,15 @@
             pltpu.VMEM((QUERY_HEADS, rows, HEAD_SIZE), jnp.float32),
             pltpu.VMEM((rows, width), jnp.bfloat16),
             pltpu.VMEM((depth if early else 256, out_width), jnp.bfloat16),
-            dma((2,)),
+            pltpu.VMEM(out_scales.shape, jnp.float32),
+            dma((3,)),
         ]
         + [dma((2, chips))] * 8
         + [dma((others, 2, chips))] * 4,
         compiler_params=pltpu.CompilerParams(
             collective_id=0, has_side_effects=True, vmem_limit_bytes=64000000
         ),
-    )(queries, kv, out_packed, scales, signs, sylvester(HEAD_SIZE))
+    )(queries, keys, values, out_packed, out_scales, signs)
 
 
 def solution(mesh):

time: 88.8 us -> 73.4 us (0.83)
  Pallas kernels: 81.7 us -> 71 us
  other arithmetic: 3.96 us -> 0 us
    pallas_call x1, Pallas kernels: 81.7 us -> 71 us  [local(): pl.pallas_call(functools.partial(kernel, n, groups, share, early), out_sh...]
    convert_element_type x3 -> x0, other arithmetic: 2.22 us -> none  [the longest x1 0.83 us: local(): scales = out_scales.astype(jnp.float32)]
    concatenate x1 -> x0, other arithmetic: 1.74 us -> none  [local(): kv = jnp.concatenate([keys, values], axis=1)]
    unnamed x3 -> x1, local copies, waits for them, and re-layouts: 2.29 us -> 2.29 us
where the time goes in v2:
time: 73.4 us; the launch traced here: 73.3 us
  Pallas kernels  71 us (97%)
  local copies, waits for them, and re-layouts  2.29 us (3%)
    pallas_call x1, Pallas kernels, local(): pl.pallas_call(functools.partial(kernel, n, groups, share, early), out_sh...  71 us
    unnamed x1, local copies, waits for them, and re-layouts  2.29 us

profile of v2, /device:TPU:17, one launch (start us, length us, event | category | flops | bytes accessed | tf_op | source)
XLA Modules:
  0.0 73.3 jit_solution(5199449441625835268)
XLA Ops:
  0.0 71.0 %shard_map.64 = bf16[128,4096]{1,0:T(8,128)(2,1)} custom-call(bf16[128,4096]{1,0:T(8,128)(2,1)} %q_ref.1, bf16[128,512]{1,0:T(8,128)(2,1)} %k_ref.1, bf16[128,512]{1,0:T(8,128)(2,1)} %v_ref.1, s32[256,512]{1,0:T(8,128)} %packed_ref.1, bf16[32,4096]{1,0:T(8,128)(2,1)} %scales_ref.1, s32[32,128]{1,0:T(8,128)} %bitcast.1), custom_call_target="tpu_custom_call" | custom-call | tf_op jit(solution)/shard_map/pallas_call | solution.py:431
  71.0 2.3 %copy.8 = bf16[128,4096]{1,0:T(8,128)(2,1)} copy(bf16[128,4096]{1,0:T(8,128)(2,1)} %shard_map.64) | data formatting | bytes 2097152
